TPU v7x, 256 devices: a whole 4x4x8 slice. The times are simulated.
256 devices in a mesh: leaf: 16 (over y, x), blk: 16 (over z, core).
Axes of the slice: x: 4, y: 4, z: 8, core: 2. Of those that a mesh axis runs over, the one named last changes fastest.
Arguments:
- leaf_rhs: bfloat16 [81920, 256], P(('leaf', 'blk')), may hold values from -6 to 6
- leaf_inverse: bfloat16 [81920, 5120], P(('leaf', 'blk')), may hold values from -0.078125 to 0.078125
- leaf_lower: bfloat16 [32768, 5120], P(('leaf', 'blk')), may hold values from -0.078125 to 0.078125
- sep_rhs: bfloat16 [4, 16384, 256], P(None, ('leaf', 'blk')), may hold values from -6 to 6
- sep_inverse: bfloat16 [16384, 30720], P(('leaf', 'blk'))
- sep_lower: bfloat16 [32768, 14336], P(('leaf', 'blk'))
- slot_map: int32 [4, 256, 2], P(None, ('leaf', 'blk')), may hold values from 0 to 5, as said below
Outputs:
- leaf_solution: bfloat16 [81920, 256], P(('leaf', 'blk'))
- sep_solution: bfloat16 [4, 16384, 256], P(None, ('leaf', 'blk'))
Inputs may be any that keep to these rules, and one draw needn't show every extreme that they name: For every level below the top, slot_map[h-1, q] holds two different numbers of 0 to 5; at the top level it holds 0 and 1 in some order.
All inputs are finite; a program needn't handle non-finite values.
Results may differ from a plain program's by a relative error of at most 0.015.
Values may be sent and summed in bfloat16 or wider, within the bound.
A program may use at most 128 MiB of HBM per device.

v0:
```python
import jax
import jax.numpy as jnp
from jax import lax
from jax.sharding import PartitionSpec as P


def partner(value, axis, apart):
    mask = 2**apart
    pairs = [(source, source ^ mask) for source in range(lax.axis_size(axis))]
    return lax.ppermute(value, axis, pairs)


def from_everyone(shard, axis):
    length = lax.axis_size(axis)
    return lax.all_to_all(
        jnp.broadcast_to(shard[None], (length, *shard.shape)), axis, 0, 0, tiled=True
    )


def laid_out(blocks, dim):
    blocks = jnp.moveaxis(blocks, 0, dim)
    shape = blocks.shape
    return blocks.reshape(*shape[:dim], shape[dim] * shape[dim + 1], *shape[dim + 2 :])


def gather_directly(shard, axis, dim):
    blocks = from_everyone(shard, axis)
    return laid_out(blocks, dim)


def pair_merge(mine, partner_rows, bit_index):
    upper_bit = jnp.bitwise_and(jnp.right_shift(lax.axis_index("leaf"), bit_index), 1)
    lower_half = jnp.where(upper_bit == 1, partner_rows, mine)
    upper_half = jnp.where(upper_bit == 1, mine, partner_rows)
    return jnp.concatenate([lower_half, upper_half], axis=0)


def group_rows(pieces, height):
    joined = pieces
    for bit_index in range(height):
        partner_rows = partner(joined, "leaf", bit_index)
        joined = pair_merge(joined, partner_rows, bit_index)
    spread = lax.all_gather(joined, "blk", axis=0, tiled=True)
    spread = spread.reshape(lax.axis_size("blk"), 2**height, pieces.shape[0], pieces.shape[1])
    return jnp.transpose(spread, (1, 0, 2, 3)).reshape(-1, pieces.shape[1])


def on_device(leaf_rhs, leaf_inverse, leaf_lower, sep_rhs, sep_inverse, sep_lower, slot_map):
    columns = leaf_rhs.shape[1]
    levels = sep_rhs.shape[0]
    pivots = sep_rhs.shape[1]
    base_width = pivots * lax.axis_size("blk")
    section = leaf_inverse
    leaf_solution = jnp.dot(
        section, gather_directly(leaf_rhs, "blk", 0), preferred_element_type=jnp.float32
    ).astype(jnp.bfloat16)
    section = leaf_lower
    update = -jnp.dot(
        section, gather_directly(leaf_solution, "blk", 0), preferred_element_type=jnp.float32
    )
    solutions = []
    for height in range(1, levels + 1):
        at_root = height == levels
        front_slots = 1 if at_root else 3
        slot_rows = update.reshape(2, pivots, columns)
        onehot = (
            slot_map[height - 1, 0][:, None]
            == jnp.arange(2 * front_slots, dtype=jnp.int32)[None, :]
        ).astype(jnp.float32)
        mixed = jnp.einsum("st,spr->tpr", onehot, slot_rows, precision=lax.Precision.HIGHEST)
        received = partner(mixed[front_slots:].astype(jnp.bfloat16), "leaf", height - 1).astype(
            jnp.float32
        )
        front_rows = mixed[:front_slots] + received
        pivot_front = (sep_rhs[height - 1].astype(jnp.float32) + front_rows[0]).astype(jnp.bfloat16)
        width_now = base_width * 2**height
        offset = base_width * (2**height - 2)
        gathered = group_rows(pivot_front, height)
        solved = jnp.dot(
            sep_inverse[:, offset : offset + width_now],
            gathered,
            preferred_element_type=jnp.float32,
        ).astype(jnp.bfloat16)
        solutions.append(solved)
        if not at_root:
            spread = group_rows(solved, height)
            product = jnp.dot(
                sep_lower[:, offset : offset + width_now],
                spread,
                preferred_element_type=jnp.float32,
            )
            update = front_rows[1:].reshape(2 * pivots, columns) - product
    return (leaf_solution, jnp.stack(solutions))


def solution(mesh):
    return jax.shard_map(
        on_device,
        mesh=mesh,
        in_specs=(
            P(("leaf", "blk"), None),
            P(("leaf", "blk"), None),
            P(("leaf", "blk"), None),
            P(None, ("leaf", "blk"), None),
            P(("leaf", "blk"), None),
            P(("leaf", "blk"), None),
            P(None, ("leaf", "blk"), None),
        ),
        out_specs=(P(("leaf", "blk"), None), P(None, ("leaf", "blk"), None)),
        check_vma=False,
    )
```

profile of v0, /device:TPU:1, one launch (start us, length us, event | category | flops | bytes accessed | tf_op | source)
XLA Modules:
  0.0 590.2 jit_solution(4690270651904076409)
XLA Ops:
  8.5 71.9 %all_to_all.10 = bf16[16,320,256]{2,1,0:T(8,128)(2,1)S(1)} all-to-all(bf16[16,320,256]{2,1,0:T(8,128)(2,1)S(1)} %broadcast_in_dim.4), channel_id=1, replica_groups=mesh['leaf'=16,'blk'=16] {'blk'}, dimensions={0} | all-to-all | bytes 5242880 | tf_op jit(solution)/shard_map/all_to_all | solution.py:15
  83.2 3.8 all-to-all-start.1
  87.2 58.6 %all-to-all-done.1 = bf16[16,320,256]{2,1,0:T(8,128)(2,1)S(1)} async-done(((bf16[16,320,256]{2,1,0:T(8,128)(2,1)}), bf16[16,320,256]{2,1,0:T(8,128)(2,1)S(1)}, u32[]{:S(2)}, u32[]{:S(2)}) %all-to-all-start.1) | async-done | bytes 2621472 | tf_op jit(solution)/shard_map/all_to_all | solution.py:15
  156.0 41.3 %all-gather.8.cloned.1.call-done = bf16[2048,256]{1,0:T(8,128)(2,1)} async-done(((bf16[128,256]{1,0:T(8,128)(2,1)}), bf16[2048,256]{1,0:T(8,128)(2,1)}) %all-gather.8.cloned.1.call-update) | async-done | bytes 1048592 | tf_op jit(solution)/shard_map/all_gather | solution.py:43
  203.5 38.2 %all-gather.10.cloned.1.call-done = bf16[2048,256]{1,0:T(8,128)(2,1)} async-done(((bf16[128,256]{1,0:T(8,128)(2,1)}), bf16[2048,256]{1,0:T(8,128)(2,1)}) %all-gather.10.cloned.1.call-update) | async-done | bytes 1048592 | tf_op jit(solution)/shard_map/all_gather | solution.py:43
  245.1 2.8 collective-permute-start.3
  247.9 2.8 collective-permute-done.3
  253.7 2.8 collective-permute-start.5
  259.2 41.3 %all-gather.12.cloned.1.call-done = bf16[4096,256]{1,0:T(8,128)(2,1)} async-done(((bf16[256,256]{1,0:T(8,128)(2,1)}), bf16[4096,256]{1,0:T(8,128)(2,1)}) %all-gather.12.cloned.1.call-update) | async-done | bytes 2097168 | tf_op jit(solution)/shard_map/all_gather | solution.py:43
  306.7 2.8 collective-permute-start.7
  312.1 40.2 %all-gather.14.cloned.1.call-done = bf16[4096,256]{1,0:T(8,128)(2,1)} async-done(((bf16[256,256]{1,0:T(8,128)(2,1)}), bf16[4096,256]{1,0:T(8,128)(2,1)}) %all-gather.14.cloned.1.call-update) | async-done | bytes 2097168 | tf_op jit(solution)/shard_map/all_gather | solution.py:43
  357.8 2.8 collective-permute-done.8
  363.8 2.8 collective-permute-start.10
  373.3 44.7 %all-gather.16.cloned.1.call-done = bf16[8192,256]{1,0:T(8,128)(2,1)} async-done(((bf16[512,256]{1,0:T(8,128)(2,1)}), bf16[8192,256]{1,0:T(8,128)(2,1)}) %all-gather.16.cloned.1.call-update) | async-done | bytes 4194320 | tf_op jit(solution)/shard_map/all_gather | solution.py:43
  425.5 2.8 collective-permute-start.13
  435.0 44.0 %all-gather.18.cloned.1.call-done = bf16[8192,256]{1,0:T(8,128)(2,1)} async-done(((bf16[512,256]{1,0:T(8,128)(2,1)}), bf16[8192,256]{1,0:T(8,128)(2,1)}) %all-gather.18.cloned.1.call-update) | async-done | bytes 4194320 | tf_op jit(solution)/shard_map/all_gather | solution.py:43
  479.0 2.7 copy.34
  483.5 2.8 collective-permute-start.15
  490.8 2.8 collective-permute-start.17
  499.5 2.8 collective-permute-start.19
  502.3 5.4 collective-permute-done.19
  508.7 60.0 %all-gather.20.cloned.1.call-done = bf16[16384,256]{1,0:T(8,128)(2,1)} async-done(((bf16[1024,256]{1,0:T(8,128)(2,1)}), bf16[16384,256]{1,0:T(8,128)(2,1)}) %all-gather.20.cloned.1.call-update) | async-done | bytes 8388624 | tf_op jit(solution)/shard_map/all_gather | solution.py:43
  568.7 8.4 %copy.38 = bf16[16,16,64,256]{3,2,0,1:T(8,128)(2,1)} copy(bf16[16,16,64,256]{3,2,1,0:T(8,128)(2,1)} %bitcast.105) | data formatting | bytes 16777216 | tf_op jit(solution)/shard_map/reshape | solution.py:44
  577.1 5.6 fusion.10
  (138 shorter events, 81.5 us)
Async XLA Ops:
  83.2 62.7 %all-to-all-start.1 = ((bf16[16,320,256]{2,1,0:T(8,128)(2,1)}), bf16[16,320,256]{2,1,0:T(8,128)(2,1)S(1)}, u32[]{:S(2)}, u32[]{:S(2)}) async-start(bf16[16,320,256]{2,1,0:T(8,128)(2,1)} %broadcast_in_dim.5), calls=%async_computation.1 | async-start | bytes 5242880 | tf_op jit(solution)/shard_map/all_to_all | solution.py:15
  87.0 110.3 %all-gather.8.cloned.1.call-start = ((), (), s32[]{:S(2)}) async-start(), calls=%async_computation.2 | async-start | bytes 1114112 | tf_op jit(solution)/shard_map/all_gather | solution.py:43
  148.3 3.9 collective-permute-start
  152.4 2.9 collective-permute-start.1
  155.9 85.8 %all-gather.10.cloned.1.call-start = ((), (), s32[]{:S(2)}) async-start(), calls=%async_computation.3 | async-start | bytes 1114112 | tf_op jit(solution)/shard_map/all_gather | solution.py:43
  203.4 97.1 %all-gather.12.cloned.1.call-start = ((), (), s32[]{:S(2)}) async-start(), calls=%async_computation.4 | async-start | bytes 2228224 | tf_op jit(solution)/shard_map/all_gather | solution.py:43
  245.1 5.7 collective-permute-start.3
  250.8 2.9 collective-permute-start.4
  253.7 4.7 collective-permute-start.5
  259.1 93.2 %all-gather.14.cloned.1.call-start = ((), (), s32[]{:S(2)}) async-start(), calls=%async_computation.5 | async-start | bytes 2228224 | tf_op jit(solution)/shard_map/all_gather | solution.py:43
  306.7 4.7 collective-permute-start.7
  312.1 106.0 %all-gather.16.cloned.1.call-start = ((), (), s32[]{:S(2)}) async-start(), calls=%async_computation.6 | async-start | bytes 4456448 | tf_op jit(solution)/shard_map/all_gather | solution.py:43
  356.5 4.2 collective-permute-start.8
  360.7 3.0 collective-permute-start.9
  363.8 4.7 collective-permute-start.10
  368.5 3.9 collective-permute-start.11
  373.3 105.7 %all-gather.18.cloned.1.call-start = ((), (), s32[]{:S(2)}) async-start(), calls=%async_computation.7 | async-start | bytes 4456448 | tf_op jit(solution)/shard_map/all_gather | solution.py:43
  425.5 4.7 collective-permute-start.13
  430.2 3.9 collective-permute-start.14
  434.9 133.8 %all-gather.20.cloned.1.call-start = ((), (), s32[]{:S(2)}) async-start(), calls=%async_computation.8 | async-start | bytes 8912896 | tf_op jit(solution)/shard_map/all_gather | solution.py:43
  483.5 4.4 collective-permute-start.15
  490.8 4.7 collective-permute-start.17
  495.5 3.9 collective-permute-start.18
  499.5 8.2 %collective-permute-start.19 = (bf16[512,256]{1,0:T(8,128)(2,1)S(1)}, bf16[512,256]{1,0:T(8,128)(2,1)S(1)}, u32[]{:S(2)}, u32[]{:S(2)}) collective-permute-start(bf16[512,256]{1,0:T(8,128)(2,1)S(1)} %pad_maximum_fusion.3), channel_id=1, source_target_pairs={{0,128},{16,144},{32,160},{48,176},{64,192},{80,208},{96,224},{112... | collective-permute-start | bytes 786440 | tf_op jit(solution)/shard_map/ppermute | solution.py:10
  (15 other events, 393.4 us)
Sparse Core Ops, SparseCore 0:
  156.0 41.1 all-gather.7
  203.5 38.2 all-gather.9
  259.2 41.1 all-gather.11
  312.2 40.1 all-gather.13
  373.4 44.6 all-gather.15
  435.0 43.8 all-gather.17
  508.8 59.8 all-gather.19
where the time goes:
time: 591 us; the launch traced here: 590 us
  waiting for transfers between devices  412 us (70%)
  blocking collectives  71.9 us (12%)
  starting transfers between devices  42 us (7%)
  local copies, waits for them, and re-layouts  24.3 us (4%)
  matrix products  19 us (3%)
  between operations  14.7 us (2%)
  other arithmetic  6.32 us (1%)
    all_gather x7, waiting for transfers between devices, group_rows(): spread = lax.all_gather(joined, 'blk', axis=0, tiled=True)  310 us
    all_to_all x1, blocking collectives, from_everyone(): lax.all_to_all(jnp.broadcast_to(shard[None], (length, *shard.shape)), axi...  71.9 us
    all_to_all x1, waiting for transfers between devices, from_everyone(): lax.all_to_all(jnp.broadcast_to(shard[None], (length, *shard.shape)), axi...  58.6 us
    ppermute x20, waiting for transfers between devices, partner(): return lax.ppermute(value, axis, pairs)  43.5 us
    ppermute x20, starting transfers between devices, partner(): return lax.ppermute(value, axis, pairs)  38 us
    reshape x7, local copies, waits for them, and re-layouts, group_rows(): spread.reshape(lax.axis_size('blk'), 2 ** height, pieces.shape[0], pieces...  19.8 us
  transfers between devices with their start and end apart: 28, of which 28 were waited for; matrix products, arithmetic and copies ran while one was open for 0% of the time, Pallas kernels for 0%

commit v1 on v0

v1 whole, which is shorter than its diff:
```python
import functools

import jax
import jax.numpy as jnp
from jax import lax
from jax.experimental import pallas as pl
from jax.experimental.pallas import tpu as pltpu
from jax.sharding import PartitionSpec as P

MESH = pl.DeviceIdType.MESH
F32 = jnp.float32
BF16 = jnp.bfloat16
CORES = 2
CHUNK = 64


def flipped(index, mask):
    result = index
    bit = 1
    while bit <= mask:
        if mask & bit:
            result = result + (bit - 2 * bit * lax.rem(lax.div(index, bit), 2))
        bit *= 2
    return result


def take(ref, sem):
    pltpu.make_async_copy(ref, ref, sem).wait()


def rows(start, count):
    return pl.ds(pl.multiple_of(start, count), count)


def kernel(
    sizes,
    leaf_rhs,
    leaf_inverse,
    leaf_lower,
    sep_rhs,
    sep_inverse,
    sep_lower,
    slot_map,
    leaf_out,
    sep_out,
    inv_v,
    low_v,
    rhs_v,
    a_v,
    l_v,
    x_leaf,
    acc,
    x_sep,
    part_own,
    part_send,
    part_recv,
    update,
    swap_send,
    swap_recv,
    kept,
    load_sem,
    out_sem,
    ring_sem,
    leaf_sib_sem,
    leaf_send_sem,
    z_sem,
    sib_sem,
    gather_send_sem,
    part_recv_sem,
    part_send_sem,
    swap_recv_sem,
    swap_send_sem,
    bulk_recv_sem,
    bulk_send_sem,
):
    n_leaf, n_blk, levels = sizes
    nz = n_blk // CORES
    half = nz // 2
    leaf = lax.axis_index("leaf")
    blk = lax.axis_index("blk")
    z = lax.div(blk, CORES)
    core = lax.rem(blk, CORES)
    sibling = (leaf, flipped(blk, 1))
    leaf_rows, columns = leaf_rhs.shape
    chunks = leaf_rows // CHUNK
    piv = sep_rhs.shape[1]
    base = piv * n_blk

    def at_z(distance):
        return lax.rem(z + (distance + nz), nz)

    loads = [
        pltpu.make_async_copy(
            leaf_rhs, x_leaf[0].at[rows(blk * leaf_rows, leaf_rows)], load_sem.at[0]
        ),
        pltpu.make_async_copy(leaf_inverse, inv_v, load_sem.at[1]),
        pltpu.make_async_copy(leaf_lower, low_v, load_sem.at[2]),
        pltpu.make_async_copy(sep_rhs, rhs_v, load_sem.at[3]),
    ]
    own_a, own_l = [], []
    for h in range(1, levels + 1):
        offset = base * (2**h - 2) + base * lax.rem(leaf, 2**h)
        cols = pl.ds(pl.multiple_of(offset, base), base)
        own_a.append(
            pltpu.make_async_copy(
                sep_inverse.at[:, cols], a_v[h - 1].at[pl.ds(0, piv)], load_sem.at[2 + 2 * h]
            )
        )
        if h < levels:
            own_l.append(
                pltpu.make_async_copy(
                    sep_lower.at[:, cols],
                    l_v[h - 1].at[pl.ds(0, 2 * piv)],
                    load_sem.at[3 + 2 * h],
                )
            )
    for copy in loads + own_a + own_l:
        copy.start()

    barrier = pltpu.get_barrier_semaphore()
    peers = [sibling]
    peers += [(leaf, at_z(d) * CORES + core) for d in range(1, nz)]
    peers += [(flipped(leaf, m), blk) for m in range(1, n_leaf)]
    for peer in peers:
        pl.semaphore_signal(barrier, inc=1, device_id=peer, device_id_type=MESH)
    pl.semaphore_wait(barrier, len(peers))

    def send(src, dst, send_sem, recv_sem, device):
        pltpu.make_async_remote_copy(
            src_ref=src,
            dst_ref=dst,
            send_sem=send_sem,
            recv_sem=recv_sem,
            device_id=device,
            device_id_type=MESH,
        ).start()

    def send_blocks(kind, h, masks):
        source = sep_inverse if kind == 0 else sep_lower
        target = a_v[h - 1] if kind == 0 else l_v[h - 1]
        count = piv if kind == 0 else 2 * piv
        index = 2 * (h - 1) + kind
        for m in masks:
            peer = flipped(leaf, m)
            offset = base * (2**h - 2) + base * lax.rem(peer, 2**h)
            send(
                source.at[:, pl.ds(pl.multiple_of(offset, base), base)],
                target.at[pl.ds(m * count, count)],
                bulk_send_sem.at[index],
                bulk_recv_sem.at[index],
                (peer, blk),
            )

    def wait_blocks(kind, h):
        target = a_v[h - 1] if kind == 0 else l_v[h - 1]
        count = piv if kind == 0 else 2 * piv
        (own_a if kind == 0 else own_l)[h - 1].wait()
        take(
            target.at[pl.ds(count, count * (2**h - 1))],
            bulk_recv_sem.at[2 * (h - 1) + kind],
        )

    def leaf_gather(phase, multiply, after_start):
        x = x_leaf[phase]
        send_sem = leaf_send_sem.at[phase]

        def chunk_at(slot, chunk):
            return x.at[rows((slot * CORES + core) * leaf_rows + chunk * CHUNK, CHUNK)]

        def hop(way, step, chunk):
            sign = 1 if way == 0 else -1
            block = chunk_at(at_z(-sign * (step - 1)), chunk)
            send(
                block,
                block,
                send_sem,
                ring_sem.at[phase, way, step - 1, chunk],
                (leaf, at_z(sign) * CORES + core),
            )

        def to_sibling(slot, sem_index, chunk):
            block = chunk_at(slot, chunk)
            send(block, block, send_sem, leaf_sib_sem.at[phase, sem_index], sibling)

        def arrived(way, step, chunk):
            sign = 1 if way == 0 else -1
            slot = at_z(-sign * step)
            take(chunk_at(slot, chunk), ring_sem.at[phase, way, step - 1, chunk])
            to_sibling(slot, (nz - step) if way == 0 else step, chunk)

        def each(first, last, body):
            def run(chunk, carry):
                body(chunk)
                return carry

            lax.fori_loop(first, last, run, 0)

        split = (chunks + 1) // 2

        def begin(chunk):
            hop(0, 1, chunk)
            hop(1, 1, chunk)
            to_sibling(z, 0, chunk)

        each(0, chunks, begin)
        after_start()

        def finish(distance):
            take(x.at[rows(0, leaf_rows)], leaf_sib_sem.at[phase, distance % nz])
            multiply(at_z(distance))

        finish(0)
        for step in range(1, half):
            if step + 1 < half:

                def both(chunk, step=step):
                    for way in (0, 1):
                        arrived(way, step, chunk)
                        hop(way, step + 1, chunk)

                each(0, chunks, both)
            else:

                def low(chunk, step=step):
                    arrived(0, step, chunk)
                    hop(0, step + 1, chunk)
                    arrived(1, step, chunk)

                def high(chunk, step=step):
                    arrived(1, step, chunk)
                    hop(1, step + 1, chunk)
                    arrived(0, step, chunk)

                each(0, split, low)
                each(split, chunks, high)
            finish(-step)
            finish(step)
        each(0, split, lambda chunk: arrived(0, half, chunk))
        each(split, chunks, lambda chunk: arrived(1, half, chunk))
        finish(half)

    def leaf_gather_sent(phase):
        total = chunks * (2 * nz - 1) * CHUNK
        take(x_leaf[phase].at[pl.ds(0, total)], leaf_send_sem.at[phase])

    chip_rows = leaf_rows * CORES

    loads[0].wait()

    def multiply_inverse(slot):
        span = rows(slot * chip_rows, chip_rows)
        acc[...] += jnp.dot(
            inv_v[:, span], x_leaf[0][span, :], preferred_element_type=F32
        )

    def multiply_lower(slot):
        span = rows(slot * chip_rows, chip_rows)
        update[...] -= jnp.dot(
            low_v[:, span], x_leaf[1][span, :], preferred_element_type=F32
        )

    def first_bulk():
        for h in (1, 2):
            if h <= levels:
                send_blocks(0, h, range(1, 2**h))
                if h < levels:
                    send_blocks(1, h, range(1, 2**h))
        acc[...] = jnp.zeros_like(acc)
        loads[1].wait()

    def second_bulk():
        if levels >= 3:
            send_blocks(0, 3, range(1, 8))
        update[...] = jnp.zeros_like(update)
        loads[2].wait()

    leaf_gather(0, multiply_inverse, first_bulk)
    own_leaf = rows(blk * leaf_rows, leaf_rows)
    x_leaf[1][own_leaf, :] = acc[...].astype(BF16)
    leaf_gather(1, multiply_lower, second_bulk)
    out_copies = [
        pltpu.make_async_copy(x_leaf[1].at[own_leaf], leaf_out, out_sem.at[0])
    ]
    out_copies[0].start()

    def gather(g, after_start):
        x = x_sep[g]

        def block(slot):
            return x.at[rows((slot * CORES + core) * piv, piv)]

        near = sorted(range(1, nz), key=lambda d: min(d, nz - d))
        for d in reversed(near):
            send(
                block(z),
                block(z),
                gather_send_sem.at[g],
                z_sem.at[g, d],
                (leaf, at_z(d) * CORES + core),
            )
        send(block(z), block(z), gather_send_sem.at[g], sib_sem.at[g], sibling)
        after_start()
        for d in near:
            slot = at_z(-d)
            take(block(slot), z_sem.at[g, d])
            send(block(slot), block(slot), gather_send_sem.at[g], sib_sem.at[g], sibling)
        take(x.at[pl.ds(0, nz * piv)], sib_sem.at[g])

    def gather_sent(g):
        take(x_sep[g].at[pl.ds(0, (2 * nz - 1) * piv)], gather_send_sem.at[g])

    def products(g, matrix, count, h):
        members = 2**h
        per = max(1, min(members, 256 // count))
        out, own = part_send[g], part_own.at[pl.ds(0, count)]
        x = x_sep[g]
        for first in reversed(range(0, members, per)):
            span = pl.ds(first * count, per * count)
            value = jnp.dot(matrix[span, :], x[...], preferred_element_type=F32)
            out[span, :] = value.astype(BF16)
            if first == 0:
                own[...] = value[:count]
            for m in range(max(first, 1), first + per):
                slot = pl.ds(m * count, count)
                send(
                    out.at[slot],
                    part_recv[g].at[slot],
                    part_send_sem.at[g],
                    part_recv_sem.at[g],
                    (flipped(leaf, m), blk),
                )
        take(part_recv[g].at[pl.ds(count, (members - 1) * count)], part_recv_sem.at[g])
        total = own[...]
        for m in range(1, members):
            total += part_recv[g][pl.ds(m * count, count), :].astype(F32)
        return total

    def products_sent(g, count, h):
        take(part_send[g].at[pl.ds(count, (2**h - 1) * count)], part_send_sem.at[g])

    later = {}
    if levels >= 4:
        later = {
            0: lambda: send_blocks(1, 3, range(1, 4)),
            1: lambda: send_blocks(1, 3, range(4, 8)),
            2: lambda: send_blocks(0, 4, range(1, 6)),
            3: lambda: send_blocks(0, 4, range(6, 11)),
            4: lambda: send_blocks(0, 4, range(11, 16)),
        }

    loads[3].wait()
    own_row = rows(blk * piv, piv)
    for h in range(1, levels + 1):
        at_root = h == levels
        slots = 1 if at_root else 3
        g = 2 * (h - 1)
        partner = (flipped(leaf, 2 ** (h - 1)), blk)

        def mixed(t):
            total = None
            for s in (0, 1):
                weight = jnp.where(slot_map[h - 1, 0, s] == t, 1.0, 0.0).astype(F32)
                term = update[pl.ds(s * piv, piv), :] * weight
                total = term if total is None else total + term
            return total

        def swap(index, start, count):
            span = pl.ds(start, count)
            send(
                swap_send[h - 1].at[span],
                swap_recv[h - 1].at[span],
                swap_send_sem.at[h - 1, index],
                swap_recv_sem.at[h - 1, index],
                partner,
            )

        swap_send[h - 1][pl.ds(0, piv), :] = mixed(slots).astype(BF16)
        swap(0, 0, piv)
        if not at_root:
            for t in (1, 2):
                swap_send[h - 1][pl.ds(t * piv, piv), :] = mixed(slots + t).astype(BF16)
            swap(1, piv, 2 * piv)
            for t in (1, 2):
                kept[pl.ds((t - 1) * piv, piv), :] = mixed(t)
        own_front = mixed(0)
        take(swap_recv[h - 1].at[pl.ds(0, piv)], swap_recv_sem.at[h - 1, 0])
        front = own_front + swap_recv[h - 1][pl.ds(0, piv), :].astype(F32)
        x_sep[g][own_row, :] = (rhs_v[h - 1].astype(F32) + front).astype(BF16)
        gather(g, later.get(g, lambda: None))
        wait_blocks(0, h)
        solved = products(g, a_v[h - 1], piv, h).astype(BF16)
        last = g + 1
        x_sep[last][own_row, :] = solved
        out_copies.append(
            pltpu.make_async_copy(
                x_sep[last].at[own_row], sep_out.at[h - 1], out_sem.at[h]
            )
        )
        out_copies[-1].start()
        if not at_root:
            gather(last, later.get(last, lambda: None))
            wait_blocks(1, h)
            product = products(last, l_v[h - 1], 2 * piv, h)
            take(swap_recv[h - 1].at[pl.ds(piv, 2 * piv)], swap_recv_sem.at[h - 1, 1])
            update[...] = (
                kept[...] + swap_recv[h - 1][pl.ds(piv, 2 * piv), :].astype(F32)
            ) - product

    for phase in (0, 1):
        leaf_gather_sent(phase)
    for h in range(1, levels + 1):
        g = 2 * (h - 1)
        gather_sent(g)
        products_sent(g, piv, h)
        take(a_v[h - 1].at[pl.ds(piv, piv * (2**h - 1))], bulk_send_sem.at[g])
        take(swap_send[h - 1].at[pl.ds(0, piv)], swap_send_sem.at[h - 1, 0])
        if h < levels:
            gather_sent(g + 1)
            products_sent(g + 1, 2 * piv, h)
            take(l_v[h - 1].at[pl.ds(2 * piv, 2 * piv * (2**h - 1))], bulk_send_sem.at[g + 1])
            take(swap_send[h - 1].at[pl.ds(piv, 2 * piv)], swap_send_sem.at[h - 1, 1])
    for copy in out_copies:
        copy.wait()


def on_device(sizes, leaf_rhs, leaf_inverse, leaf_lower, sep_rhs, sep_inverse, sep_lower, slot_map):
    n_leaf, n_blk, levels = sizes
    leaf_rows, columns = leaf_rhs.shape
    chunks = leaf_rows // CHUNK
    nz = n_blk // CORES
    piv = sep_rhs.shape[1]
    base = piv * n_blk
    gathers = 2 * levels - 1

    def level_of(g):
        return g // 2 + 1

    def count_of(g):
        return piv * (1 + g % 2)

    vmem, dma = pltpu.VMEM, pltpu.SemaphoreType.DMA
    parts = [vmem((count_of(g) * 2 ** level_of(g), columns), BF16) for g in range(gathers)]
    any_space = pl.BlockSpec(memory_space=pl.ANY)
    return pl.pallas_call(
        functools.partial(kernel, sizes),
        out_shape=(
            jax.ShapeDtypeStruct((leaf_rows, columns), BF16),
            jax.ShapeDtypeStruct((levels, piv, columns), BF16),
        ),
        in_specs=[any_space] * 6 + [pl.BlockSpec(memory_space=pltpu.SMEM)],
        out_specs=(any_space, any_space),
        scratch_shapes=[
            vmem(leaf_inverse.shape, BF16),
            vmem(leaf_lower.shape, BF16),
            vmem(sep_rhs.shape, BF16),
            [vmem((piv * 2**h, base), BF16) for h in range(1, levels + 1)],
            [vmem((2 * piv * 2**h, base), BF16) for h in range(1, levels)],
            [vmem((leaf_rows * n_blk, columns), BF16) for _ in range(2)],
            vmem((leaf_rows, columns), F32),
            [vmem((base, columns), BF16) for _ in range(gathers + 1)],
            vmem((2 * piv, columns), F32),
            parts,
            parts,
            vmem((2 * piv, columns), F32),
            [vmem((3 * piv, columns), BF16) for _ in range(levels)],
            [vmem((3 * piv, columns), BF16) for _ in range(levels)],
            vmem((2 * piv, columns), F32),
            dma((3 + 2 * levels,)),
            dma((1 + levels,)),
            dma((2, 2, nz // 2, chunks)),
            dma((2, nz)),
            dma((2,)),
            dma((gathers, nz)),
            dma((gathers,)),
            dma((gathers,)),
            dma((gathers,)),
            dma((gathers,)),
            dma((levels, 2)),
            dma((levels, 2)),
            dma((gathers,)),
            dma((gathers,)),
        ],
        compiler_params=pltpu.CompilerParams(
            collective_id=0, has_side_effects=True, vmem_limit_bytes=60 * 2**20
        ),
    )(leaf_rhs, leaf_inverse, leaf_lower, sep_rhs, sep_inverse, sep_lower, slot_map)


def solution(mesh):
    n_leaf, n_blk = mesh.shape["leaf"], mesh.shape["blk"]
    sizes = (n_leaf, n_blk, n_leaf.bit_length() - 1)
    return jax.shard_map(
        functools.partial(on_device, sizes),
        mesh=mesh,
        in_specs=(
            P(("leaf", "blk"), None),
            P(("leaf", "blk"), None),
            P(("leaf", "blk"), None),
            P(None, ("leaf", "blk"), None),
            P(("leaf", "blk"), None),
            P(("leaf", "blk"), None),
            P(None, ("leaf", "blk"), None),
        ),
        out_specs=(P(("leaf", "blk"), None), P(None, ("leaf", "blk"), None)),
        check_vma=False,
    )
```

time: 591 us -> 180 us (0.30)
  waiting for transfers between devices: 412 us -> 0 us
  Pallas kernels: 0 us -> 175 us
  blocking collectives: 71.9 us -> 0 us
  starting transfers between devices: 42 us -> 0 us
  local copies, waits for them, and re-layouts: 24.3 us -> 4.5 us
  matrix products: 19 us -> 0 us
  between operations: 14.7 us -> 0.64 us
  other arithmetic: 6.32 us -> 0 us
    all_gather x7 -> x0, waiting for transfers between devices: 310 us -> none  [group_rows(): spread = lax.all_gather(joined, 'blk', axis=0, tiled=True)]
    pallas_call x0 -> x1, Pallas kernels: none -> 175 us  [on_device(): pl.pallas_call(functools.partial(kernel, sizes), out_shape=(jax.ShapeDtyp...]
    all_to_all x1 -> x0, blocking collectives: 71.9 us -> none  [from_everyone(): lax.all_to_all(jnp.broadcast_to(shard[None], (length, *shard.shape)), axi...]
    all_to_all x1 -> x0, waiting for transfers between devices: 58.6 us -> none  [from_everyone(): lax.all_to_all(jnp.broadcast_to(shard[None], (length, *shard.shape)), axi...]
    ppermute x20 -> x0, waiting for transfers between devices: 43.5 us -> none  [partner(): return lax.ppermute(value, axis, pairs)]
    ppermute x20 -> x0, starting transfers between devices: 38 us -> none  [partner(): return lax.ppermute(value, axis, pairs)]
    reshape x7 -> x0, local copies, waits for them, and re-layouts: 19.8 us -> none  [group_rows(): spread.reshape(lax.axis_size('blk'), 2 ** height, pieces.shape[0], pieces...]
    dot_general x13 -> x0, matrix products: 19 us -> none  [the longest x4 10.4 us: on_device(): jnp.dot(sep_inverse[:, offset:offset + width_now], gathered, preferred_el...]
  transfers between devices with their start and end apart: 28 -> 0, of which waited for: 28 -> 0; matrix products, arithmetic and copies ran while one was open for 0% -> 0% of each run, Pallas kernels for 0% -> 0%
where the time goes in v1:
time: 180 us
  Pallas kernels  175 us (97%)
  local copies, waits for them, and re-layouts  4.5 us (2%)
    pallas_call x1, Pallas kernels, on_device(): pl.pallas_call(functools.partial(kernel, sizes), out_shape=(jax.ShapeDtyp...  175 us
    unnamed x3, local copies, waits for them, and re-layouts  4.5 us

profile of v1, /device:TPU:1, one launch (start us, length us, event | category | flops | bytes accessed | tf_op | source)
XLA Modules:
  0.0 180.3 jit_solution(11904771790793278093)
XLA Ops:
  0.6 1.3 copy.9.slot_map
  2.0 175.2 %shard_map.86 = (bf16[320,256]{1,0:T(8,128)(2,1)}, bf16[4,64,256]{2,1,0:T(8,128)(2,1)}) custom-call(bf16[320,256]{1,0:T(8,128)(2,1)} %leaf_rhs.1, bf16[320,5120]{1,0:T(8,128)(2,1)} %leaf_inverse.1, bf16[128,5120]{1,0:T(8,128)(2,1)} %leaf_lower.1, bf16[4,64,256]{2,1,0:T(8,128)(2,1)} %sep_rhs.1, bf16[64,30720]{1,0:T(8,128)(2,1)} %sep_inverse.1, ...), custom_call_target="tpu_custom_call" | custom-call | tf_op jit(solution)/shard_map/pallas_call | solution.py:444
  177.2 1.6 copy.12
  178.8 1.6 copy.13

commit v2 on v0

v2 whole, which is shorter than its diff:
```python
import functools

import jax
import jax.numpy as jnp
from jax import lax
from jax.experimental import pallas as pl
from jax.experimental.pallas import tpu as pltpu
from jax.sharding import PartitionSpec as P

MESH = pl.DeviceIdType.MESH
F32 = jnp.float32
BF16 = jnp.bfloat16
CORES = 2
NX = 4
CHUNK = 64
CHAINS = 2
LEAD = 0.0
LEAF_HOP = 2.9
SIBLING = 0.0
LEAF_SIBLING = 0.0
GATHER = 5.5
SWAP = 2.6
PARTS_A = (2.6, 3.3, 4.5, 6.0)
PARTS_L = (3.0, 4.0, 6.0)
BULK_A3 = 6.0
GATHER_X = (0.5, 0.0)
BULK_ROOM = (8, 8, 8, 8, 0, 0, 0)


def flipped(index, mask):
    result = index
    bit = 1
    while bit <= mask:
        if mask & bit:
            result = result + (bit - 2 * bit * lax.rem(lax.div(index, bit), 2))
        bit *= 2
    return result


def wide_level(h, levels):
    return h == levels


def masks_of(h, levels):
    return [m for m in range(2**h) if not wide_level(h, levels) or m % NX == 0]


def take(ref, sem):
    pltpu.make_async_copy(ref, ref, sem).wait()


def rows(start, count):
    return pl.ds(pl.multiple_of(start, count), count)


def kernel(
    sizes,
    leaf_rhs,
    leaf_inverse,
    leaf_lower,
    sep_rhs,
    sep_inverse,
    sep_lower,
    slot_map,
    leaf_out,
    sep_out,
    inv_v,
    low_v,
    rhs_v,
    map_s,
    a_v,
    l_v,
    chains,
    load_sem,
    bulk_recv_sem,
    bulk_send_sem,
):
    n_leaf, n_blk, levels = sizes
    nz = n_blk // CORES
    half = nz // 2
    leaf = lax.axis_index("leaf")
    blk = lax.axis_index("blk")
    z = lax.div(blk, CORES)
    core = lax.rem(blk, CORES)
    sibling = (leaf, flipped(blk, 1))
    leaf_rows, columns = leaf_rhs.shape
    width = columns // CHAINS
    chunks = leaf_rows // CHUNK
    chip_rows = leaf_rows * CORES
    piv = sep_rhs.shape[1]
    base = piv * n_blk
    own_leaf = rows(blk * leaf_rows, leaf_rows)

    def own_row(h):
        if wide_level(h, levels):
            return rows(lax.rem(leaf, NX) * base + blk * piv, piv)
        return rows(blk * piv, piv)

    def columns_for(h, member):
        index = lax.rem(member, 2**h)
        span = base
        if wide_level(h, levels):
            index, span = lax.div(index, NX), base * NX
        return pl.ds(pl.multiple_of(base * (2**h - 2) + span * index, base), span)

    def at_z(distance):
        return lax.rem(z + (distance + nz), nz)

    def columns_of(c):
        return pl.ds(c * width, width)

    loads = {}

    def load(key, source, target):
        loads[key] = pltpu.make_async_copy(source, target, load_sem.at[len(loads)])
        loads[key].start()

    waited = set()

    def loaded(key):
        if key not in waited:
            waited.add(key)
            loads[key].wait()
            if key[0] in ("a", "l"):
                while any(item[:2] == key for _, item in bulk):
                    send_block(*bulk.pop(0)[1])
                with jax.named_scope(f"blocks{key[0]}{key[1]}"):
                    wait_blocks(*key)

    for c in range(CHAINS):
        load(("rhs", c), leaf_rhs.at[:, columns_of(c)], chains[c]["x_leaf"][0].at[own_leaf])
    load(("inverse",), leaf_inverse, inv_v)
    load(("lower",), leaf_lower, low_v)
    load(("sep_rhs",), sep_rhs, rhs_v)
    load(("map",), slot_map, map_s)
    for h in range(1, levels + 1):
        own = columns_for(h, leaf)
        load(("a", h), sep_inverse.at[:, own], a_v[h - 1].at[pl.ds(0, piv)])
        if h < levels:
            load(("l", h), sep_lower.at[:, own], l_v[h - 1].at[pl.ds(0, 2 * piv)])

    barrier = pltpu.get_barrier_semaphore()
    peers = [sibling]
    peers += [(leaf, at_z(d) * CORES + core) for d in range(1, nz)]
    peers += [(flipped(leaf, m), blk) for m in range(1, n_leaf)]
    for peer in peers:
        pl.semaphore_signal(barrier, inc=1, device_id=peer, device_id_type=MESH)
    for c in range(CHAINS):
        loaded(("rhs", c))
    with jax.named_scope("entry"):
        pl.semaphore_wait(barrier, len(peers))

    def send(src, dst, send_sem, recv_sem, device):
        pltpu.make_async_remote_copy(
            src_ref=src,
            dst_ref=dst,
            send_sem=send_sem,
            recv_sem=recv_sem,
            device_id=device,
            device_id_type=MESH,
        ).start()

    def matrix_of(kind, h):
        if kind == "a":
            return sep_inverse, a_v[h - 1], piv, 2 * (h - 1)
        return sep_lower, l_v[h - 1], 2 * piv, 2 * (h - 1) + 1

    def send_block(kind, h, m, first, size):
        source, target, count, index = matrix_of(kind, h)
        peer = flipped(leaf, m)
        size = min(size, count)
        slot = masks_of(h, levels).index(m)
        send(
            source.at[pl.ds(first, size), columns_for(h, peer)],
            target.at[pl.ds(slot * count + first, size)],
            bulk_send_sem.at[index],
            bulk_recv_sem.at[index],
            (peer, blk),
        )

    def wait_blocks(kind, h):
        source, target, count, index = matrix_of(kind, h)
        others = len(masks_of(h, levels)) - 1
        take(target.at[pl.ds(count, count * others)], bulk_recv_sem.at[index])

    def blocks_beside(g):
        room = BULK_ROOM[g]
        while bulk and room > 0:
            item = bulk.pop(0)[1]
            send_block(*item)
            room -= (0, 1, 2, 1)[item[2] % 4]

    def each(first, last, body):
        def run(chunk, carry):
            body(chunk)
            return carry

        lax.fori_loop(first, last, run, 0)

    def leaf_gather(c, phase, multiply):
        own = chains[c]
        x = own["x_leaf"][phase]
        send_sem = own["leaf_send_sem"].at[phase]

        def chunk_at(slot, chunk):
            return x.at[rows((slot * CORES + core) * leaf_rows + chunk * CHUNK, CHUNK)]

        def hop(way, step, chunk):
            sign = 1 if way == 0 else -1
            block = chunk_at(at_z(-sign * (step - 1)), chunk)
            send(
                block,
                block,
                send_sem,
                own["ring_sem"].at[phase, way, step - 1, chunk],
                (leaf, at_z(sign) * CORES + core),
            )

        def to_sibling(slot, sem_index, chunk):
            block = chunk_at(slot, chunk)
            send(block, block, send_sem, own["leaf_sib_sem"].at[phase, sem_index], sibling)

        def arrived(way, step, chunk):
            sign = 1 if way == 0 else -1
            slot = at_z(-sign * step)
            take(chunk_at(slot, chunk), own["ring_sem"].at[phase, way, step - 1, chunk])
            to_sibling(slot, (nz - step) if way == 0 else step, chunk)

        split = (chunks + c) // 2 if CHAINS > 1 else (chunks + 1) // 2

        def begin(chunk):
            hop(0, 1, chunk)
            hop(1, 1, chunk)
            to_sibling(z, 0, chunk)

        def finish(distance):
            take(x.at[rows(0, leaf_rows)], own["leaf_sib_sem"].at[phase, distance % nz])
            multiply(at_z(distance), distance == 0)

        each(0, chunks, begin)
        yield LEAF_HOP
        for step in range(1, half):
            with jax.named_scope(f"leaf{phase}c{c}s{step}"):
                if step + 1 < half:

                    def both(chunk, step=step):
                        for way in (0, 1):
                            arrived(way, step, chunk)
                            hop(way, step + 1, chunk)

                    each(0, chunks, both)
                else:

                    def low(chunk, step=step):
                        arrived(0, step, chunk)
                        hop(0, step + 1, chunk)
                        arrived(1, step, chunk)

                    def high(chunk, step=step):
                        arrived(1, step, chunk)
                        hop(1, step + 1, chunk)
                        arrived(0, step, chunk)

                    each(0, split, low)
                    each(split, chunks, high)
            with jax.named_scope(f"leafm{phase}c{c}s{step}"):
                if step == 1:
                    finish(0)
                else:
                    finish(1 - step)
                    finish(step - 1)
            yield LEAF_HOP
        with jax.named_scope(f"leaf{phase}c{c}s{half}"):
            each(0, split, lambda chunk: arrived(0, half, chunk))
            each(split, chunks, lambda chunk: arrived(1, half, chunk))
        if half > 1:
            finish(1 - half)
            finish(half - 1)
        else:
            finish(0)
        yield LEAF_SIBLING
        with jax.named_scope(f"leafm{phase}c{c}s{half}"):
            finish(half)

    def gather(c, g, h, name):
        own = chains[c]
        wide = wide_level(h, levels)
        x = own["x_sep"][g]
        part = lax.rem(leaf, NX) * base if wide else 0

        def block(slot, start=part):
            return x.at[rows(start + (slot * CORES + core) * piv, piv)]

        def push(ref, sem, device):
            send(ref, ref, own["gather_send_sem"].at[g], sem, device)

        def to_sibling(ref):
            push(ref, own["sib_sem"].at[g], sibling)

        near = sorted(range(1, nz), key=lambda d: min(d, nz - d))
        halves = ([0] + near[: nz // 2 - 1], near[nz // 2 - 1 :])

        def along_x(d):
            if wide:
                for m in (1, 3, 2):
                    if m < NX:
                        sem = own["x_sem"].at[m, 0 if d in halves[0] else 1]
                        push(block(at_z(-d)), sem, (flipped(leaf, m), blk))

        for d in reversed(near):
            push(block(z), own["z_sem"].at[g, d], (leaf, at_z(d) * CORES + core))
        to_sibling(block(z))
        along_x(0)
        if c == CHAINS - 1:
            blocks_beside(g)

        yield GATHER
        with jax.named_scope(f"far{name}c{c}"):
            for d in near:
                take(block(at_z(-d)), own["z_sem"].at[g, d])
                along_x(d)
                to_sibling(block(at_z(-d)))
        if wide:
            for half_index in (0, 1):
                yield GATHER_X[half_index]
                with jax.named_scope(f"x{half_index}{name}c{c}"):
                    for m in (1, 3, 2):
                        if m < NX:
                            take(
                                x.at[pl.ds(0, len(halves[half_index]) * piv)],
                                own["x_sem"].at[m, half_index],
                            )
                            start = lax.rem(flipped(leaf, m), NX) * base
                            for d in halves[half_index]:
                                to_sibling(block(at_z(-d), start))
        yield SIBLING
        with jax.named_scope(f"sib{name}c{c}"):
            take(x.at[pl.ds(0, nz * piv * (NX if wide else 1))], own["sib_sem"].at[g])

    def products(c, g, matrix, count, h):
        own = chains[c]
        masks = masks_of(h, levels)
        members = len(masks)
        per = max(1, min(members, 256 // count))
        out, mine = own["part_send"][g], own["part_own"].at[pl.ds(0, count)]
        x = own["x_sep"][g]
        for first in reversed(range(0, members, per)):
            span = pl.ds(first * count, per * count)
            value = jnp.dot(matrix[span, :], x[...], preferred_element_type=F32)
            out[span, :] = value.astype(BF16)
            if first == 0:
                mine[...] = value[:count]
            for m in range(max(first, 1), first + per):
                slot = pl.ds(m * count, count)
                send(
                    out.at[slot],
                    own["part_recv"][g].at[slot],
                    own["part_send_sem"].at[g],
                    own["part_recv_sem"].at[g],
                    (flipped(leaf, masks[m]), blk),
                )

    def summed(c, g, count, h, name):
        own = chains[c]
        members = len(masks_of(h, levels))
        with jax.named_scope(f"parts{name}c{c}"):
            take(
                own["part_recv"][g].at[pl.ds(count, (members - 1) * count)],
                own["part_recv_sem"].at[g],
            )
        total = own["part_own"][pl.ds(0, count), :]
        for m in range(1, members):
            total += own["part_recv"][g][pl.ds(m * count, count), :].astype(F32)
        return total

    out_copies = []

    def write(source, target, sem):
        out_copies.append(pltpu.make_async_copy(source, target, sem))
        out_copies[-1].start()

    def chain(c):
        own = chains[c]
        cols = columns_of(c)
        acc, update, kept = own["acc"], own["update"], own["kept"]

        def multiply_inverse(slot, first):
            loaded(("inverse",))
            span = rows(slot * chip_rows, chip_rows)
            value = jnp.dot(inv_v[:, span], own["x_leaf"][0][span, :], preferred_element_type=F32)
            acc[...] = value if first else acc[...] + value

        def multiply_lower(slot, first):
            loaded(("lower",))
            span = rows(slot * chip_rows, chip_rows)
            value = jnp.dot(low_v[:, span], own["x_leaf"][1][span, :], preferred_element_type=F32)
            update[...] = -value if first else update[...] - value

        yield from leaf_gather(c, 0, multiply_inverse)
        own["x_leaf"][1][own_leaf, :] = acc[...].astype(BF16)
        yield from leaf_gather(c, 1, multiply_lower)
        write(own["x_leaf"][1].at[own_leaf], leaf_out.at[:, cols], own["out_sem"].at[0])

        for h in range(1, levels + 1):
            at_root = h == levels
            slots = 1 if at_root else 3
            g = 2 * (h - 1)
            partner = (flipped(leaf, 2 ** (h - 1)), blk)
            swap_send, swap_recv = own["swap_send"][h - 1], own["swap_recv"][h - 1]
            loaded(("map",))
            loaded(("sep_rhs",))

            def mixed(t):
                total = None
                for s in (0, 1):
                    weight = jnp.where(map_s[s, h - 1] == t, 1.0, 0.0).astype(F32)
                    term = update[pl.ds(s * piv, piv), :] * weight
                    total = term if total is None else total + term
                return total

            def swap(index, start, count):
                span = pl.ds(start, count)
                send(
                    swap_send.at[span],
                    swap_recv.at[span],
                    own["swap_send_sem"].at[h - 1, index],
                    own["swap_recv_sem"].at[h - 1, index],
                    partner,
                )

            swap_send[pl.ds(0, piv), :] = mixed(slots).astype(BF16)
            swap(0, 0, piv)
            if not at_root:
                for t in (1, 2):
                    swap_send[pl.ds(t * piv, piv), :] = mixed(slots + t).astype(BF16)
                swap(1, piv, 2 * piv)
                for t in (1, 2):
                    kept[pl.ds((t - 1) * piv, piv), :] = mixed(t)
            own["part_own"][pl.ds(0, piv), :] = mixed(0)
            yield SWAP
            with jax.named_scope(f"swap{h}c{c}"):
                take(swap_recv.at[pl.ds(0, piv)], own["swap_recv_sem"].at[h - 1, 0])
            front = own["part_own"][pl.ds(0, piv), :] + swap_recv[pl.ds(0, piv), :].astype(F32)
            own["x_sep"][g][own_row(h), :] = (rhs_v[h - 1, :, cols].astype(F32) + front).astype(BF16)
            yield from gather(c, g, h, f"A{h}")
            with jax.named_scope(f"productA{h}c{c}"):
                loaded(("a", h))
                products(c, g, a_v[h - 1], piv, h)
            yield PARTS_A[h - 1]
            solved = summed(c, g, piv, h, f"A{h}").astype(BF16)
            last = g + 1
            solved_row = rows(blk * piv, piv)
            own["x_sep"][last][solved_row, :] = solved
            write(
                own["x_sep"][last].at[solved_row], sep_out.at[h - 1, :, cols], own["out_sem"].at[h]
            )
            if not at_root:
                yield from gather(c, last, h, f"L{h}")
                with jax.named_scope(f"productL{h}c{c}"):
                    loaded(("l", h))
                    products(c, last, l_v[h - 1], 2 * piv, h)
                yield PARTS_L[h - 1]
                product = summed(c, last, 2 * piv, h, f"L{h}")
                take(swap_recv.at[pl.ds(piv, 2 * piv)], own["swap_recv_sem"].at[h - 1, 1])
                update[...] = (
                    kept[...] + swap_recv[pl.ds(piv, 2 * piv), :].astype(F32)
                ) - product

    bulk = bulk_plan(levels, piv)
    running = {c: chain(c) for c in range(CHAINS)}
    ready = {c: c * LEAD for c in range(CHAINS)}
    now = 0.0
    while running:
        c = min(running, key=lambda k: ready[k])
        now = max(now, ready[c])
        try:
            ready[c] = now + next(running[c])
        except StopIteration:
            del running[c]
        while bulk and bulk[0][0] <= now:
            send_block(*bulk.pop(0)[1])

    for c in range(CHAINS):
        own = chains[c]
        for phase in (0, 1):
            total = chunks * (2 * nz - 1) * CHUNK
            take(own["x_leaf"][phase].at[pl.ds(0, total)], own["leaf_send_sem"].at[phase])
        for h in range(1, levels + 1):
            for kind in (0, 1):
                if kind == 1 and h == levels:
                    continue
                g = 2 * (h - 1) + kind
                count = piv * (1 + kind)
                blocks = 2 * nz * (NX if wide_level(h, levels) else 1) - 1
                others = len(masks_of(h, levels)) - 1
                take(own["x_sep"][g].at[pl.ds(0, blocks * piv)], own["gather_send_sem"].at[g])
                take(
                    own["part_send"][g].at[pl.ds(count, others * count)],
                    own["part_send_sem"].at[g],
                )
                span = pl.ds(kind * piv, count)
                take(own["swap_send"][h - 1].at[span], own["swap_send_sem"].at[h - 1, kind])
    for h in range(1, levels + 1):
        for kind in ("a", "l"):
            if kind == "l" and h == levels:
                continue
            source, target, count, index = matrix_of(kind, h)
            others = len(masks_of(h, levels)) - 1
            take(target.at[pl.ds(count, count * others)], bulk_send_sem.at[index])
    for copy in out_copies:
        copy.wait()


def bulk_plan(levels, piv):
    def pieces(kind, h, masks, size):
        count = piv if kind == "a" else 2 * piv
        size = min(size, count)
        known = masks_of(h, levels)
        return [
            (kind, h, m, f, size) for m in masks if m in known for f in range(0, count, size)
        ]

    def at(when, items):
        return [(when, item) for item in items]

    plan = []
    for h in range(1, min(levels, 3)):
        for kind in ("a", "l"):
            plan += at(0.0, pieces(kind, h, (1, 3, 2), 2 * piv))
    plan += at(0.0, pieces("a", levels, [NX * m for m in (1, 3, 2)], 2 * piv))
    if levels > 3:
        plan += at(0.0, pieces("a", 3, (4,), 2 * piv))
        plan += at(BULK_A3, pieces("a", 3, (1, 3, 2, 5, 7, 6), 2 * piv))
        plan += at(BULK_A3, pieces("l", 3, (4,), 2 * piv))
        plan += at(1e9, pieces("l", 3, (1, 3, 2, 5, 7, 6), piv // 2))
    return plan


def put_out(leaf_in, sep_in, leaf_out, sep_out, sem):
    copies = [
        pltpu.make_async_copy(leaf_in, leaf_out, sem.at[0]),
        pltpu.make_async_copy(sep_in, sep_out, sem.at[1]),
    ]
    for copy in copies:
        copy.start()
    for copy in copies:
        copy.wait()


def on_device(sizes, leaf_rhs, leaf_inverse, leaf_lower, sep_rhs, sep_inverse, sep_lower, slot_map):
    n_leaf, n_blk, levels = sizes
    leaf_rows, columns = leaf_rhs.shape
    chunks = leaf_rows // CHUNK
    nz = n_blk // CORES
    piv = sep_rhs.shape[1]
    base = piv * n_blk
    gathers = 2 * levels - 1
    slots = slot_map[:, 0, :].T

    def level_of(g):
        return g // 2 + 1

    def count_of(g):
        return piv * (1 + g % 2)

    vmem, dma = pltpu.VMEM, pltpu.SemaphoreType.DMA
    width = columns // CHAINS

    def parts():
        return [
            vmem((count_of(g) * len(masks_of(level_of(g), levels)), width), BF16)
            for g in range(gathers)
        ]

    def swaps():
        return [vmem((3 * piv, width), BF16) for _ in range(levels)]

    def scratch_of_chain():
        return {
            "x_leaf": [vmem((leaf_rows * n_blk, width), BF16) for _ in range(2)],
            "acc": vmem((leaf_rows, width), F32),
            "x_sep": [
                vmem((base * (NX if g < gathers and wide_level(level_of(g), levels) else 1), width), BF16)
                for g in range(gathers + 1)
            ],
            "part_own": vmem((2 * piv, width), F32),
            "part_send": parts(),
            "part_recv": parts(),
            "update": vmem((2 * piv, width), F32),
            "swap_send": swaps(),
            "swap_recv": swaps(),
            "kept": vmem((2 * piv, width), F32),
            "out_sem": dma((1 + levels,)),
            "ring_sem": dma((2, 2, nz // 2, chunks)),
            "leaf_sib_sem": dma((2, nz)),
            "leaf_send_sem": dma((2,)),
            "z_sem": dma((gathers, nz)),
            "x_sem": dma((NX, 2)),
            "sib_sem": dma((gathers,)),
            "gather_send_sem": dma((gathers,)),
            "part_recv_sem": dma((gathers,)),
            "part_send_sem": dma((gathers,)),
            "swap_recv_sem": dma((levels, 2)),
            "swap_send_sem": dma((levels, 2)),
        }

    any_space = pl.BlockSpec(memory_space=pl.ANY)
    leaf_out, sep_out = pl.pallas_call(
        functools.partial(kernel, sizes),
        out_shape=(
            jax.ShapeDtypeStruct((leaf_rows, columns), BF16),
            jax.ShapeDtypeStruct((levels, piv, columns), BF16),
        ),
        in_specs=[any_space] * 7,
        out_specs=(pl.BlockSpec(memory_space=pltpu.VMEM),) * 2,
        scratch_shapes=[
            vmem(leaf_inverse.shape, BF16),
            vmem(leaf_lower.shape, BF16),
            vmem(sep_rhs.shape, BF16),
            pltpu.SMEM(slots.shape, jnp.int32),
            [
                vmem(
                    (piv * len(masks_of(h, levels)), base * 2**h // len(masks_of(h, levels))), BF16
                )
                for h in range(1, levels + 1)
            ],
            [vmem((2 * piv * 2**h, base), BF16) for h in range(1, levels)],
            [scratch_of_chain() for _ in range(CHAINS)],
            dma((CHAINS + 4 + 2 * levels,)),
            dma((gathers,)),
            dma((gathers,)),
        ],
        compiler_params=pltpu.CompilerParams(
            collective_id=0, has_side_effects=True, vmem_limit_bytes=60 * 2**20
        ),
    )(leaf_rhs, leaf_inverse, leaf_lower, sep_rhs, sep_inverse, sep_lower, slots)
    return pl.pallas_call(
        put_out,
        out_shape=(
            jax.ShapeDtypeStruct((leaf_rows, columns), BF16),
            jax.ShapeDtypeStruct((levels, piv, columns), BF16),
        ),
        in_specs=[pl.BlockSpec(memory_space=pltpu.VMEM)] * 2,
        out_specs=(any_space, any_space),
        scratch_shapes=[dma((2,))],
    )(leaf_out, sep_out)


def solution(mesh):
    n_leaf, n_blk = mesh.shape["leaf"], mesh.shape["blk"]
    sizes = (n_leaf, n_blk, n_leaf.bit_length() - 1)
    return jax.shard_map(
        functools.partial(on_device, sizes),
        mesh=mesh,
        in_specs=(
            P(("leaf", "blk"), None),
            P(("leaf", "blk"), None),
            P(("leaf", "blk"), None),
            P(None, ("leaf", "blk"), None),
            P(("leaf", "blk"), None),
            P(("leaf", "blk"), None),
            P(None, ("leaf", "blk"), None),
        ),
        out_specs=(P(("leaf", "blk"), None), P(None, ("leaf", "blk"), None)),
        check_vma=False,
    )
```

time: 591 us -> 157 us (0.27)
  waiting for transfers between devices: 412 us -> 0 us
  Pallas kernels: 0 us -> 156 us
  blocking collectives: 71.9 us -> 0 us
  starting transfers between devices: 42 us -> 0 us
  local copies, waits for them, and re-layouts: 24.3 us -> 0 us
  matrix products: 19 us -> 0 us
  between operations: 14.7 us -> 0.8 us
  other arithmetic: 6.32 us -> 0 us
    all_gather x7 -> x0, waiting for transfers between devices: 310 us -> none  [group_rows(): spread = lax.all_gather(joined, 'blk', axis=0, tiled=True)]
    pallas_call x0 -> x2, Pallas kernels: none -> 156 us  [the longest x1 154 us: on_device(): pl.pallas_call(functools.partial(kernel, sizes), out_shape=(jax.ShapeDtyp...]
    all_to_all x1 -> x0, blocking collectives: 71.9 us -> none  [from_everyone(): lax.all_to_all(jnp.broadcast_to(shard[None], (length, *shard.shape)), axi...]
    all_to_all x1 -> x0, waiting for transfers between devices: 58.6 us -> none  [from_everyone(): lax.all_to_all(jnp.broadcast_to(shard[None], (length, *shard.shape)), axi...]
    ppermute x20 -> x0, waiting for transfers between devices: 43.5 us -> none  [partner(): return lax.ppermute(value, axis, pairs)]
    ppermute x20 -> x0, starting transfers between devices: 38 us -> none  [partner(): return lax.ppermute(value, axis, pairs)]
    reshape x7 -> x0, local copies, waits for them, and re-layouts: 19.8 us -> none  [group_rows(): spread.reshape(lax.axis_size('blk'), 2 ** height, pieces.shape[0], pieces...]
    dot_general x13 -> x0, matrix products: 19 us -> none  [the longest x4 10.4 us: on_device(): jnp.dot(sep_inverse[:, offset:offset + width_now], gathered, preferred_el...]
  transfers between devices with their start and end apart: 28 -> 0, of which waited for: 28 -> 0; matrix products, arithmetic and copies ran while one was open for 0% -> 0% of each run, Pallas kernels for 0% -> 0%
where the time goes in v2:
time: 157 us
  Pallas kernels  156 us (99%)
    pallas_call x1, Pallas kernels, on_device(): pl.pallas_call(functools.partial(kernel, sizes), out_shape=(jax.ShapeDtyp...  154 us

profile of v2, /device:TPU:1, one launch (start us, length us, event | category | flops | bytes accessed | tf_op | source)
XLA Modules:
  0.0 157.0 jit_solution(4676041030045829265)
XLA Ops:
  0.6 154.5 %shard_map.86 = (bf16[320,256]{1,0:T(8,128)(2,1)}, bf16[4,64,256]{2,1,0:T(8,128)(2,1)}) custom-call(bf16[320,256]{1,0:T(8,128)(2,1)} %leaf_rhs.1, bf16[320,5120]{1,0:T(8,128)(2,1)} %leaf_inverse.1, bf16[128,5120]{1,0:T(8,128)(2,1)} %leaf_lower.1, bf16[4,64,256]{2,1,0:T(8,128)(2,1)} %sep_rhs.1, bf16[64,30720]{1,0:T(8,128)(2,1)} %sep_inverse.1, ...), custom_call_target="tpu_custom_call" | custom-call | tf_op jit(solution)/shard_map/pallas_call | solution.py:608
  155.1 1.7 %shard_map.87 = (bf16[320,256]{1,0:T(8,128)(2,1)}, bf16[4,64,256]{2,1,0:T(8,128)(2,1)}) custom-call(bf16[320,256]{1,0:T(8,128)(2,1)} %get-tuple-element.4.leaf_in, bf16[4,64,256]{2,1,0:T(8,128)(2,1)} %get-tuple-element.5.sep_in), custom_call_target="tpu_custom_call" | custom-call | tf_op jit(solution)/shard_map/pallas_call | solution.py:637

commit v3 on v2

--- a/solution.py
+++ b/solution.py
@@ -12,19 +12,20 @@
 BF16 = jnp.bfloat16
 CORES = 2
 NX = 4
-CHUNK = 64
+SEND_GATHERS = 3
+CHUNK = 160
 CHAINS = 2
 LEAD = 0.0
 LEAF_HOP = 2.9
 SIBLING = 0.0
-LEAF_SIBLING = 0.0
+LEAF_SIBLING = 1.0
 GATHER = 5.5
 SWAP = 2.6
 PARTS_A = (2.6, 3.3, 4.5, 6.0)
 PARTS_L = (3.0, 4.0, 6.0)
 BULK_A3 = 6.0
 GATHER_X = (0.5, 0.0)
-BULK_ROOM = (8, 8, 8, 8, 0, 0, 0)
+BULK_ROOM = (8, 4, 7, 7, 6, 4, 0)
 
 
 def flipped(index, mask):
@@ -43,6 +44,10 @@
 
 def masks_of(h, levels):
     return [m for m in range(2**h) if not wide_level(h, levels) or m % NX == 0]
+
+
+def send_group(g):
+    return 2 + g // SEND_GATHERS
 
 
 def take(ref, sem):
@@ -200,7 +205,7 @@
     def leaf_gather(c, phase, multiply):
         own = chains[c]
         x = own["x_leaf"][phase]
-        send_sem = own["leaf_send_sem"].at[phase]
+        send_sem = own["send_sem"].at[phase]
 
         def chunk_at(slot, chunk):
             return x.at[rows((slot * CORES + core) * leaf_rows + chunk * CHUNK, CHUNK)]
@@ -224,7 +229,7 @@
             sign = 1 if way == 0 else -1
             slot = at_z(-sign * step)
             take(chunk_at(slot, chunk), own["ring_sem"].at[phase, way, step - 1, chunk])
-            to_sibling(slot, (nz - step) if way == 0 else step, chunk)
+            to_sibling(slot, step, chunk)
 
         split = (chunks + c) // 2 if CHAINS > 1 else (chunks + 1) // 2
 
@@ -233,9 +238,11 @@
             hop(1, 1, chunk)
             to_sibling(z, 0, chunk)
 
-        def finish(distance):
-            take(x.at[rows(0, leaf_rows)], own["leaf_sib_sem"].at[phase, distance % nz])
-            multiply(at_z(distance), distance == 0)
+        def finish(step):
+            ways = (step,) if step in (0, half) else (-step, step)
+            take(x.at[pl.ds(0, len(ways) * leaf_rows)], own["leaf_sib_sem"].at[phase, step])
+            for distance in ways:
+                multiply(at_z(distance), distance == 0)
 
         each(0, chunks, begin)
         yield LEAF_HOP
@@ -264,20 +271,12 @@
                     each(0, split, low)
                     each(split, chunks, high)
             with jax.named_scope(f"leafm{phase}c{c}s{step}"):
-                if step == 1:
-                    finish(0)
-                else:
-                    finish(1 - step)
-                    finish(step - 1)
+                finish(step - 1)
             yield LEAF_HOP
+        finish(half - 1)
         with jax.named_scope(f"leaf{phase}c{c}s{half}"):
             each(0, split, lambda chunk: arrived(0, half, chunk))
             each(split, chunks, lambda chunk: arrived(1, half, chunk))
-        if half > 1:
-            finish(1 - half)
-            finish(half - 1)
-        else:
-            finish(0)
         yield LEAF_SIBLING
         with jax.named_scope(f"leafm{phase}c{c}s{half}"):
             finish(half)
@@ -292,23 +291,25 @@
             return x.at[rows(start + (slot * CORES + core) * piv, piv)]
 
         def push(ref, sem, device):
-            send(ref, ref, own["gather_send_sem"].at[g], sem, device)
+            send(ref, ref, own["send_sem"].at[send_group(g)], sem, device)
 
         def to_sibling(ref):
             push(ref, own["sib_sem"].at[g], sibling)
 
         near = sorted(range(1, nz), key=lambda d: min(d, nz - d))
-        halves = ([0] + near[: nz // 2 - 1], near[nz // 2 - 1 :])
+        halves = (near[: nz // 2], near[nz // 2 :])
+        x_halves = ([0] + halves[0], halves[1])
 
         def along_x(d):
             if wide:
                 for m in (1, 3, 2):
                     if m < NX:
-                        sem = own["x_sem"].at[m, 0 if d in halves[0] else 1]
+                        sem = own["x_sem"].at[m - 1, 1 if d in halves[1] else 0]
                         push(block(at_z(-d)), sem, (flipped(leaf, m), blk))
 
         for d in reversed(near):
-            push(block(z), own["z_sem"].at[g, d], (leaf, at_z(d) * CORES + core))
+            sem = own["z_sem"].at[g, 1 if d in halves[1] else 0]
+            push(block(z), sem, (leaf, at_z(d) * CORES + core))
         to_sibling(block(z))
         along_x(0)
         if c == CHAINS - 1:
@@ -316,10 +317,11 @@
 
         yield GATHER
         with jax.named_scope(f"far{name}c{c}"):
-            for d in near:
-                take(block(at_z(-d)), own["z_sem"].at[g, d])
-                along_x(d)
-                to_sibling(block(at_z(-d)))
+            for index in (0, 1):
+                take(x.at[pl.ds(0, len(halves[index]) * piv)], own["z_sem"].at[g, index])
+                for d in halves[index]:
+                    along_x(d)
+                    to_sibling(block(at_z(-d)))
         if wide:
             for half_index in (0, 1):
                 yield GATHER_X[half_index]
@@ -327,11 +329,11 @@
                     for m in (1, 3, 2):
                         if m < NX:
                             take(
-                                x.at[pl.ds(0, len(halves[half_index]) * piv)],
-                                own["x_sem"].at[m, half_index],
+                                x.at[pl.ds(0, len(x_halves[half_index]) * piv)],
+                                own["x_sem"].at[m - 1, half_index],
                             )
                             start = lax.rem(flipped(leaf, m), NX) * base
-                            for d in halves[half_index]:
+                            for d in x_halves[half_index]:
                                 to_sibling(block(at_z(-d), start))
         yield SIBLING
         with jax.named_scope(f"sib{name}c{c}"):
@@ -355,7 +357,7 @@
                 send(
                     out.at[slot],
                     own["part_recv"][g].at[slot],
-                    own["part_send_sem"].at[g],
+                    own["send_sem"].at[send_group(g)],
                     own["part_recv_sem"].at[g],
                     (flipped(leaf, masks[m]), blk),
                 )
@@ -373,12 +375,6 @@
             total += own["part_recv"][g][pl.ds(m * count, count), :].astype(F32)
         return total
 
-    out_copies = []
-
-    def write(source, target, sem):
-        out_copies.append(pltpu.make_async_copy(source, target, sem))
-        out_copies[-1].start()
-
     def chain(c):
         own = chains[c]
         cols = columns_of(c)
@@ -399,7 +395,7 @@
         yield from leaf_gather(c, 0, multiply_inverse)
         own["x_leaf"][1][own_leaf, :] = acc[...].astype(BF16)
         yield from leaf_gather(c, 1, multiply_lower)
-        write(own["x_leaf"][1].at[own_leaf], leaf_out.at[:, cols], own["out_sem"].at[0])
+        leaf_out[:, cols] = own["x_leaf"][1][own_leaf, :]
 
         for h in range(1, levels + 1):
             at_root = h == levels
@@ -423,7 +419,7 @@
                 send(
                     swap_send.at[span],
                     swap_recv.at[span],
-                    own["swap_send_sem"].at[h - 1, index],
+                    own["send_sem"].at[send_group(g)],
                     own["swap_recv_sem"].at[h - 1, index],
                     partner,
                 )
@@ -449,12 +445,9 @@
             yield PARTS_A[h - 1]
             solved = summed(c, g, piv, h, f"A{h}").astype(BF16)
             last = g + 1
-            solved_row = rows(blk * piv, piv)
-            own["x_sep"][last][solved_row, :] = solved
-            write(
-                own["x_sep"][last].at[solved_row], sep_out.at[h - 1, :, cols], own["out_sem"].at[h]
-            )
+            sep_out[h - 1, :, cols] = solved
             if not at_root:
+                own["x_sep"][last][own_row(h), :] = solved
                 yield from gather(c, last, h, f"L{h}")
                 with jax.named_scope(f"productL{h}c{c}"):
                     loaded(("l", h))
@@ -482,24 +475,21 @@
 
     for c in range(CHAINS):
         own = chains[c]
-        for phase in (0, 1):
-            total = chunks * (2 * nz - 1) * CHUNK
-            take(own["x_leaf"][phase].at[pl.ds(0, total)], own["leaf_send_sem"].at[phase])
+        total = {phase: chunks * (2 * nz - 1) * CHUNK for phase in (0, 1)}
         for h in range(1, levels + 1):
             for kind in (0, 1):
                 if kind == 1 and h == levels:
                     continue
                 g = 2 * (h - 1) + kind
                 count = piv * (1 + kind)
+                group = send_group(g)
                 blocks = 2 * nz * (NX if wide_level(h, levels) else 1) - 1
                 others = len(masks_of(h, levels)) - 1
-                take(own["x_sep"][g].at[pl.ds(0, blocks * piv)], own["gather_send_sem"].at[g])
-                take(
-                    own["part_send"][g].at[pl.ds(count, others * count)],
-                    own["part_send_sem"].at[g],
-                )
-                span = pl.ds(kind * piv, count)
-                take(own["swap_send"][h - 1].at[span], own["swap_send_sem"].at[h - 1, kind])
+                total[group] = total.get(group, 0) + blocks * piv + others * count
+                group = send_group(2 * (h - 1))
+                total[group] = total.get(group, 0) + count
+        for group, amount in total.items():
+            take(own["x_leaf"][0].at[pl.ds(0, amount)], own["send_sem"].at[group])
     for h in range(1, levels + 1):
         for kind in ("a", "l"):
             if kind == "l" and h == levels:
@@ -507,8 +497,6 @@
             source, target, count, index = matrix_of(kind, h)
             others = len(masks_of(h, levels)) - 1
             take(target.at[pl.ds(count, count * others)], bulk_send_sem.at[index])
-    for copy in out_copies:
-        copy.wait()
 
 
 def bulk_plan(levels, piv):
@@ -530,9 +518,12 @@
     plan += at(0.0, pieces("a", levels, [NX * m for m in (1, 3, 2)], 2 * piv))
     if levels > 3:
         plan += at(0.0, pieces("a", 3, (4,), 2 * piv))
-        plan += at(BULK_A3, pieces("a", 3, (1, 3, 2, 5, 7, 6), 2 * piv))
+        plan += at(BULK_A3, pieces("a", 3, (2, 6, 1, 5), 2 * piv))
         plan += at(BULK_A3, pieces("l", 3, (4,), 2 * piv))
-        plan += at(1e9, pieces("l", 3, (1, 3, 2, 5, 7, 6), piv // 2))
+        plan += at(1e9, pieces("l", 3, (3, 7), piv // 2))
+        plan += at(1e9, pieces("a", 3, (3, 7), piv // 2))
+        mixed = zip(*(pieces("l", 3, (m,), piv // 2) for m in (2, 1, 6, 5)))
+        plan += at(1e9, [item for group in mixed for item in group])
     return plan
 
 
@@ -590,18 +581,14 @@
             "swap_send": swaps(),
             "swap_recv": swaps(),
             "kept": vmem((2 * piv, width), F32),
-            "out_sem": dma((1 + levels,)),
             "ring_sem": dma((2, 2, nz // 2, chunks)),
-            "leaf_sib_sem": dma((2, nz)),
-            "leaf_send_sem": dma((2,)),
-            "z_sem": dma((gathers, nz)),
-            "x_sem": dma((NX, 2)),
+            "leaf_sib_sem": dma((2, nz // 2 + 1)),
+            "send_sem": dma((3 + (gathers - 1) // SEND_GATHERS,)),
+            "z_sem": dma((gathers, 2)),
+            "x_sem": dma((NX - 1, 2)),
             "sib_sem": dma((gathers,)),
-            "gather_send_sem": dma((gathers,)),
             "part_recv_sem": dma((gathers,)),
-            "part_send_sem": dma((gathers,)),
             "swap_recv_sem": dma((levels, 2)),
-            "swap_send_sem": dma((levels, 2)),
         }
 
     any_space = pl.BlockSpec(memory_space=pl.ANY)

time: 157 us -> 155 us (0.987)
  Pallas kernels: 156 us -> 154 us
    pallas_call x1, Pallas kernels: 154 us -> 152 us  [on_device(): pl.pallas_call(functools.partial(kernel, sizes), out_shape=(jax.ShapeDtyp...]
where the time goes in v3:
time: 155 us
  Pallas kernels  154 us (99%)
    pallas_call x1, Pallas kernels, on_device(): pl.pallas_call(functools.partial(kernel, sizes), out_shape=(jax.ShapeDtyp...  152 us

profile of v3, /device:TPU:1, one launch (start us, length us, event | category | flops | bytes accessed | tf_op | source)
XLA Modules:
  0.0 154.9 jit_solution(13636504287206251235)
XLA Ops:
  0.6 152.4 %shard_map.86 = (bf16[320,256]{1,0:T(8,128)(2,1)}, bf16[4,64,256]{2,1,0:T(8,128)(2,1)}) custom-call(bf16[320,256]{1,0:T(8,128)(2,1)} %leaf_rhs.1, bf16[320,5120]{1,0:T(8,128)(2,1)} %leaf_inverse.1, bf16[128,5120]{1,0:T(8,128)(2,1)} %leaf_lower.1, bf16[4,64,256]{2,1,0:T(8,128)(2,1)} %sep_rhs.1, bf16[64,30720]{1,0:T(8,128)(2,1)} %sep_inverse.1, ...), custom_call_target="tpu_custom_call" | custom-call | tf_op jit(solution)/shard_map/pallas_call | solution.py:595
  153.0 1.7 %shard_map.87 = (bf16[320,256]{1,0:T(8,128)(2,1)}, bf16[4,64,256]{2,1,0:T(8,128)(2,1)}) custom-call(bf16[320,256]{1,0:T(8,128)(2,1)} %get-tuple-element.4.leaf_in, bf16[4,64,256]{2,1,0:T(8,128)(2,1)} %get-tuple-element.5.sep_in), custom_call_target="tpu_custom_call" | custom-call | tf_op jit(solution)/shard_map/pallas_call | solution.py:624
